TPU v7x, 256 devices: a whole 4x4x8 slice. The times are simulated.
256 devices in a mesh: wide: 64 (over x, z_hi, y), narrow: 4 (over z_lo, core).
Axes of the slice: x: 4, y: 4, z: 8 (z_hi: 4, z_lo: 2; z = z_hi * 2 + z_lo), core: 2. Of those that a mesh axis runs over, the one named last changes fastest.
Arguments:
- coefficients: bfloat16 [512, 2, 256, 512], P(('wide', 'narrow')), may hold values from -6 to 6
- col_weights: bfloat16 [2, 512, 2, 256, 512], P(None, ('wide', 'narrow')), may hold values from -0.1875 to 0.1875
- row_weights: bfloat16 [2, 512, 2, 256, 512], P(None, 'wide'), may hold values from -0.1875 to 0.1875
Outputs:
- applied: bfloat16 [512, 2, 256, 512], P('wide', None, None, 'narrow')
All inputs are finite; a program needn't handle non-finite values.
Results may differ from a plain program's by a relative error of at most 0.0064.
Values may be sent and summed in bfloat16 or wider, within the bound.
A program may use at most 64 MiB of HBM per device.

v0:
```python
import jax
import jax.numpy as jnp
from jax import lax
from jax.sharding import PartitionSpec as P


def swapped(array, axis, apart):
    return lax.ppermute(array, axis, [(i, i ^ 1 << apart) for i in range(lax.axis_size(axis))])


def planes(weights, block):
    merged = jnp.concatenate([block[:, 0], block[:, 1]], axis=-1)
    first = jnp.einsum("kab,kbn->kan", weights[:, 0], merged, preferred_element_type=jnp.float32)
    second = jnp.einsum("kab,kbn->kan", weights[:, 1], merged, preferred_element_type=jnp.float32)
    return (first, second)


def finish(first, second, count):
    real = first[..., :count] - second[..., count:]
    imag = first[..., count:] + second[..., :count]
    return jnp.stack([real, imag], axis=1).astype(jnp.bfloat16)


def combine(coef, weights, partner, upper):
    count = coef.shape[-1]
    rank = coef.shape[2]
    own_weights = jnp.where(upper, weights[..., rank:], weights[..., :rank])
    other_weights = jnp.where(upper, weights[..., :rank], weights[..., rank:])
    own_first, own_second = planes(own_weights, coef)
    other_first, other_second = planes(other_weights, partner)
    return finish(own_first + other_first, own_second + other_second, count)


def per_device(coefficients, col_weights, row_weights):
    wide_bits = lax.axis_size("wide").bit_length() - 1
    position = lax.axis_index("wide")

    def is_upper(bit):
        return position >> bit & 1 == 1

    state = combine(coefficients, col_weights[0], swapped(coefficients, "wide", 0), is_upper(0))
    state = combine(state, col_weights[1], swapped(state, "wide", 1), is_upper(1))
    state = lax.all_to_all(state, "narrow", split_axis=3, concat_axis=0, tiled=True)
    row_sets = [row_weights[0], row_weights[1]]
    for level in range(2):
        bit = wide_bits - 2 + level
        state = combine(state, row_sets[level], swapped(state, "wide", bit), is_upper(bit))
    return state


def solution(mesh):
    placed = (
        P(("wide", "narrow"), None, None, None),
        P(None, ("wide", "narrow"), None, None, None),
        P(None, "wide", None, None, None),
    )
    return jax.shard_map(
        per_device,
        mesh=mesh,
        in_specs=placed,
        out_specs=P("wide", None, None, "narrow"),
        check_vma=False,
    )
```

profile of v0, /device:TPU:64, one launch (start us, length us, event | category | flops | bytes accessed | tf_op | source)
XLA Modules:
  0.0 132.0 jit_solution(17459165918152072332)
XLA Ops:
  0.0 2.4 %copy.21 = bf16[2,2,256,512]{3,2,0,1:T(8,128)(2,1)} copy(bf16[2,2,256,512]{3,2,1,0:T(8,128)(2,1)} %param.3) | data formatting | bytes 2097152 | tf_op args[0]
  2.4 1.6 %collective-permute-start = (bf16[2,2,256,512]{3,2,0,1:T(8,128)(2,1)}, bf16[2,2,256,512]{3,2,0,1:T(8,128)(2,1)S(1)}, u32[]{:S(2)}, u32[]{:S(2)}) collective-permute-start(bf16[2,2,256,512]{3,2,0,1:T(8,128)(2,1)} %copy.21), channel_id=1, source_target_pairs={{0,4},{4,0},{8,12},{12,8},{16,20},{20,16},{24,28},{28,24},{32,36},... | collective-permute-start | bytes 3145736 | tf_op jit(solution)/shard_map/ppermute | solution.py:8
  4.0 0.2 fusion.37
  4.2 0.2 copy_bitcast_fusion.2
  4.4 0.1 broadcast_select_fusion.4
  4.5 1.1 copy-done
  5.7 0.4 fusion.14
  6.2 0.4 fusion.15
  6.6 20.9 %collective-permute-done = bf16[2,2,256,512]{3,2,0,1:T(8,128)(2,1)S(1)} collective-permute-done((bf16[2,2,256,512]{3,2,0,1:T(8,128)(2,1)}, bf16[2,2,256,512]{3,2,0,1:T(8,128)(2,1)S(1)}, u32[]{:S(2)}, u32[]{:S(2)}) %collective-permute-start) | collective-permute-done | bytes 1048608 | tf_op jit(solution)/shard_map/ppermute | solution.py:8
  27.6 0.5 convolution_add_fusion.6
  28.1 0.5 convolution_add_fusion.7
  28.5 0.6 fusion.9
  29.1 1.1 pad_maximum_fusion.3
  30.2 3.2 %collective-permute-start.1 = (bf16[2,2,256,512]{3,2,0,1:T(8,128)(2,1)}, bf16[2,2,256,512]{3,2,0,1:T(8,128)(2,1)S(1)}, u32[]{:S(2)}, u32[]{:S(2)}) collective-permute-start(bf16[2,2,256,512]{3,2,0,1:T(8,128)(2,1)} %pad_maximum_fusion.3), channel_id=1, source_target_pairs={{0,8},{4,12},{8,0},{12,4},{16,24},{20,28},{24,16},{28,20},{32,40},... | collective-permute-start | bytes 3145736 | tf_op jit(solution)/shard_map/ppermute | solution.py:8
  33.4 0.1 broadcast_select_fusion.6
  33.4 0.4 fusion.12
  33.9 0.4 fusion.13
  34.3 21.6 %collective-permute-done.1 = bf16[2,2,256,512]{3,2,0,1:T(8,128)(2,1)S(1)} collective-permute-done((bf16[2,2,256,512]{3,2,0,1:T(8,128)(2,1)}, bf16[2,2,256,512]{3,2,0,1:T(8,128)(2,1)S(1)}, u32[]{:S(2)}, u32[]{:S(2)}) %collective-permute-start.1) | collective-permute-done | bytes 1048608 | tf_op jit(solution)/shard_map/ppermute | solution.py:8
  56.0 0.5 convolution_add_fusion.4
  56.5 0.5 convolution_add_fusion.5
  56.9 0.6 fusion.16
  57.5 0.1 pad_maximum_fusion.5
  57.6 2.1 %copy.24 = bf16[2,2,256,512]{2,0,1,3:T(2,128)(2,1)} copy(bf16[2,2,256,512]{3,2,0,1:T(8,128)(2,1)S(1)} %pad_maximum_fusion.5) | data formatting | bytes 2097152 | tf_op jit(solution)/shard_map/stack | solution.py:21
  59.7 3.5 %all-to-all-start = ((bf16[2,2,256,512]{2,0,1,3:T(2,128)(2,1)}), bf16[2,2,256,512]{2,0,1,3:T(2,128)(2,1)S(1)}, u32[]{:S(2)}, u32[]{:S(2)}) async-start(bf16[2,2,256,512]{2,0,1,3:T(2,128)(2,1)} %copy.24), calls=%async_computation | async-start | bytes 2097152 | tf_op jit(solution)/shard_map/all_to_all | solution.py:43
  63.3 3.9 %fusion.36 = (bf16[1,8,2,256,512]{4,3,2,1,0:T(8,128)(2,1)S(1)}, bf16[1,8,2,256,512]{4,3,2,1,0:T(8,128)(2,1)S(1)}) fusion(bf16[2,8,2,256,512]{4,3,2,1,0:T(8,128)(2,1)} %param.5), kind=kLoop, calls=%fused_computation.104 | loop fusion | bytes 16777216 | tf_op jit(solution)/shard_map/slice | solution.py:44
  67.1 3.8 %copy_bitcast_fusion = (bf16[8,2,256,512]{3,2,0,1:T(8,128)(2,1)}, bf16[8,2,256,512]{3,2,0,1:T(8,128)(2,1)}) fusion(bf16[1,8,2,256,512]{4,3,2,1,0:T(8,128)(2,1)S(1)} %get-tuple-element.5, bf16[1,8,2,256,512]{4,3,2,1,0:T(8,128)(2,1)S(1)} %get-tuple-element.6), kind=kLoop, calls=%fused_computation | loop fusion | bytes 16777216 | tf_op jit(solution)/shard_map/squeeze | solution.py:44
  70.9 6.7 %all-to-all-done = bf16[2,2,256,512]{2,0,1,3:T(2,128)(2,1)S(1)} async-done(((bf16[2,2,256,512]{2,0,1,3:T(2,128)(2,1)}), bf16[2,2,256,512]{2,0,1,3:T(2,128)(2,1)S(1)}, u32[]{:S(2)}, u32[]{:S(2)}) %all-to-all-start) | async-done | bytes 1048608 | tf_op jit(solution)/shard_map/all_to_all | solution.py:43
  77.7 0.2 copy.25
  77.8 1.6 %collective-permute-start.2 = (bf16[8,2,256,128]{2,3,0,1:T(8,128)(2,1)S(1)}, bf16[8,2,256,128]{2,3,0,1:T(8,128)(2,1)S(1)}, u32[]{:S(2)}, u32[]{:S(2)}) collective-permute-start(bf16[8,2,256,128]{2,3,0,1:T(8,128)(2,1)S(1)} %bitcast.101), channel_id=1, source_target_pairs={{0,64},{4,68},{8,72},{12,76},{16,80},{20,84},{24,88},{28,92},{32,9... | collective-permute-start | bytes 3145736 | tf_op jit(solution)/shard_map/ppermute | solution.py:8
  79.4 2.5 %broadcast_select_fusion = (bf16[8,2,256,256]{3,2,0,1:T(8,128)(2,1)S(1)}, bf16[8,2,256,256]{3,2,0,1:T(8,128)(2,1)S(1)}) fusion(pred[]{:T(512)S(6)} %eq.13, bf16[8,2,256,512]{3,2,0,1:T(8,128)(2,1)} %get-tuple-element.37), kind=kLoop, calls=%fused_computation.2 | loop fusion | flops 2097152 | bytes 8388609 | tf_op jit(solution)/shard_map/jit(_where)/select_n | solution.py:28
  81.9 0.1 slice_bitcast_fusion.21
  82.0 0.5 fusion.5
  82.5 0.5 fusion.10
  82.9 19.6 %collective-permute-done.2 = bf16[8,2,256,128]{2,3,0,1:T(8,128)(2,1)S(1)} collective-permute-done((bf16[8,2,256,128]{2,3,0,1:T(8,128)(2,1)S(1)}, bf16[8,2,256,128]{2,3,0,1:T(8,128)(2,1)S(1)}, u32[]{:S(2)}, u32[]{:S(2)}) %collective-permute-start.2) | collective-permute-done | bytes 1048608 | tf_op jit(solution)/shard_map/ppermute | solution.py:8
  102.6 0.5 convolution_add_fusion.2
  103.1 0.5 convolution_add_fusion.3
  103.6 0.5 fusion.4
  104.1 0.1 pad_maximum_fusion.9
  104.2 3.1 %collective-permute-start.3 = (bf16[8,2,256,128]{2,3,0,1:T(8,128)(2,1)S(1)}, bf16[8,2,256,128]{2,3,0,1:T(8,128)(2,1)S(1)}, u32[]{:S(2)}, u32[]{:S(2)}) collective-permute-start(bf16[8,2,256,128]{2,3,0,1:T(8,128)(2,1)S(1)} %pad_maximum_fusion.9), channel_id=1, source_target_pairs={{0,128},{4,132},{8,136},{12,140},{16,144},{20,148},{24,152},{28,15... | collective-permute-start | bytes 3145736 | tf_op jit(solution)/shard_map/ppermute | solution.py:8
  107.3 2.5 %broadcast_select_fusion.2 = (bf16[8,2,256,256]{3,2,0,1:T(8,128)(2,1)S(1)}, bf16[8,2,256,256]{3,2,0,1:T(8,128)(2,1)S(1)}) fusion(pred[]{:T(512)S(6)} %eq.12, bf16[8,2,256,512]{3,2,0,1:T(8,128)(2,1)} %get-tuple-element.38), kind=kLoop, calls=%fused_computation.4 | loop fusion | flops 2097152 | bytes 8388609 | tf_op jit(solution)/shard_map/jit(_where)/select_n | solution.py:28
  109.8 0.5 fusion.2
  110.3 0.5 fusion.11
  110.7 18.8 %collective-permute-done.3 = bf16[8,2,256,128]{2,3,0,1:T(8,128)(2,1)S(1)} collective-permute-done((bf16[8,2,256,128]{2,3,0,1:T(8,128)(2,1)S(1)}, bf16[8,2,256,128]{2,3,0,1:T(8,128)(2,1)S(1)}, u32[]{:S(2)}, u32[]{:S(2)}) %collective-permute-start.3) | collective-permute-done | bytes 1048608 | tf_op jit(solution)/shard_map/ppermute | solution.py:8
  129.6 0.5 convolution_add_fusion
  130.1 0.5 convolution_add_fusion.1
  130.6 0.2 fusion.18
  130.8 0.1 pad_maximum_fusion.11
  130.9 1.0 copy.30
  (8 shorter events, 0.4 us)
Async XLA Ops:
  0.0 4.0 %copy-start.1 = (bf16[2,2,2,256,512]{4,3,2,1,0:T(8,128)(2,1)S(1)}, bf16[2,2,2,256,512]{4,3,2,1,0:T(8,128)(2,1)}, u32[]{:S(2)}) copy-start(bf16[2,2,2,256,512]{4,3,2,1,0:T(8,128)(2,1)} %param.4) | copy-start | bytes 6291460
  2.4 25.1 %collective-permute-start = (bf16[2,2,256,512]{3,2,0,1:T(8,128)(2,1)}, bf16[2,2,256,512]{3,2,0,1:T(8,128)(2,1)S(1)}, u32[]{:S(2)}, u32[]{:S(2)}) collective-permute-start(bf16[2,2,256,512]{3,2,0,1:T(8,128)(2,1)} %copy.21), channel_id=1, source_target_pairs={{0,4},{4,0},{8,12},{12,8},{16,20},{20,16},{24,28},{28,24},{32,36},... | collective-permute-start | bytes 3145736 | tf_op jit(solution)/shard_map/ppermute | solution.py:8
  4.4 1.2 copy-start
  30.2 25.8 %collective-permute-start.1 = (bf16[2,2,256,512]{3,2,0,1:T(8,128)(2,1)}, bf16[2,2,256,512]{3,2,0,1:T(8,128)(2,1)S(1)}, u32[]{:S(2)}, u32[]{:S(2)}) collective-permute-start(bf16[2,2,256,512]{3,2,0,1:T(8,128)(2,1)} %pad_maximum_fusion.3), channel_id=1, source_target_pairs={{0,8},{4,12},{8,0},{12,4},{16,24},{20,28},{24,16},{28,20},{32,40},... | collective-permute-start | bytes 3145736 | tf_op jit(solution)/shard_map/ppermute | solution.py:8
  59.7 17.9 %all-to-all-start = ((bf16[2,2,256,512]{2,0,1,3:T(2,128)(2,1)}), bf16[2,2,256,512]{2,0,1,3:T(2,128)(2,1)S(1)}, u32[]{:S(2)}, u32[]{:S(2)}) async-start(bf16[2,2,256,512]{2,0,1,3:T(2,128)(2,1)} %copy.24), calls=%async_computation | async-start | bytes 2097152 | tf_op jit(solution)/shard_map/all_to_all | solution.py:43
  77.8 24.7 %collective-permute-start.2 = (bf16[8,2,256,128]{2,3,0,1:T(8,128)(2,1)S(1)}, bf16[8,2,256,128]{2,3,0,1:T(8,128)(2,1)S(1)}, u32[]{:S(2)}, u32[]{:S(2)}) collective-permute-start(bf16[8,2,256,128]{2,3,0,1:T(8,128)(2,1)S(1)} %bitcast.101), channel_id=1, source_target_pairs={{0,64},{4,68},{8,72},{12,76},{16,80},{20,84},{24,88},{28,92},{32,9... | collective-permute-start | bytes 3145736 | tf_op jit(solution)/shard_map/ppermute | solution.py:8
  104.2 25.3 %collective-permute-start.3 = (bf16[8,2,256,128]{2,3,0,1:T(8,128)(2,1)S(1)}, bf16[8,2,256,128]{2,3,0,1:T(8,128)(2,1)S(1)}, u32[]{:S(2)}, u32[]{:S(2)}) collective-permute-start(bf16[8,2,256,128]{2,3,0,1:T(8,128)(2,1)S(1)} %pad_maximum_fusion.9), channel_id=1, source_target_pairs={{0,128},{4,132},{8,136},{12,140},{16,144},{20,148},{24,152},{28,15... | collective-permute-start | bytes 3145736 | tf_op jit(solution)/shard_map/ppermute | solution.py:8
where the time goes:
time: 132 us
  waiting for transfers between devices  87.6 us (66%)
  local copies, waits for them, and re-layouts  15.4 us (12%)
  starting transfers between devices  13 us (10%)
  other arithmetic  8.39 us (6%)
  matrix products  7.42 us (6%)
    ppermute x4, waiting for transfers between devices, swapped(): lax.ppermute(array, axis, [(i, i ^ 1 << apart) for i in range(lax.axis_si...  80.9 us
    ppermute x4, starting transfers between devices, swapped(): lax.ppermute(array, axis, [(i, i ^ 1 << apart) for i in range(lax.axis_si...  9.45 us
    all_to_all x1, waiting for transfers between devices, per_device(): lax.all_to_all(state, 'narrow', split_axis=3, concat_axis=0, tiled=True)  6.72 us
    select_n x4, other arithmetic, combine(): other_weights = jnp.where(upper, weights[..., :rank], weights[..., rank:])  5.14 us
    slice x1, local copies, waits for them, and re-layouts, per_device(): row_sets = [row_weights[0], row_weights[1]]  3.87 us
    squeeze x1, local copies, waits for them, and re-layouts, per_device(): row_sets = [row_weights[0], row_weights[1]]  3.8 us
    dot_general x8, matrix products, planes(): jnp.einsum('kab,kbn->kan', weights[:, 1], merged, preferred_element_type=...  3.71 us
    dot_general x8, matrix products, planes(): jnp.einsum('kab,kbn->kan', weights[:, 0], merged, preferred_element_type=...  3.71 us
  transfers between devices with their start and end apart: 5, of which 5 were waited for; matrix products, arithmetic and copies ran while one was open for 13% of the time, Pallas kernels for 0%

commit v1 on v0

v1 whole, which is shorter than its diff:
```python
import functools

import jax
import jax.numpy as jnp
from jax import lax
from jax.experimental import pallas as pl
from jax.experimental.pallas import tpu as pltpu
from jax.sharding import PartitionSpec as P

MESH = pl.DeviceIdType.MESH
TURNS = (2, 3, 1, 0)
AHEAD = 2


def turned(index, turn):
    if turn == 0:
        return index
    if turn == 1:
        return index + 1 - 2 * (index % 2)
    if turn == 2:
        return index + 2 - 4 * (index // 2)
    return 3 - index


def multiply(weights, block, store):
    merged = block[...].reshape(weights.shape[2], block.shape[2])
    half = merged.shape[1] // 2
    first = jnp.dot(weights[0], merged, preferred_element_type=jnp.float32)
    second = jnp.dot(weights[1], merged, preferred_element_type=jnp.float32)
    real = first[:, :half] - second[:, half:]
    imag = first[:, half:] + second[:, :half]
    store(real.astype(jnp.bfloat16), imag.astype(jnp.bfloat16))


def events(chunks, moved):
    timed = []
    for c in range(chunks):
        one = 2 * c + 0.6 if c else 1.6
        two = 3.6 + 2 * c
        if c == chunks - 1:
            two -= 1
        relay = two + 1.7 if c < moved - 2 else two + 0.6
        three = (relay if c < moved else two) + 1.7
        four = three + 2
        timed += [(one, 1, c), (two, 2, c), (three, 4, c), (four, 5, c)]
        if c < moved:
            timed.append((relay, 3, c))
    return [(stage, c) for _, stage, c in sorted(timed)]


def kernel(wide_bits, coef, colw, roww, out, x1, x2, x3, x4, stage, done, cw, rw,
           coef_sem, cw_sem, rw_sem, out_sem, send, recv):
    w = lax.axis_index("wide")
    n = lax.axis_index("narrow")
    nodes = coef.shape[0]
    turns = len(TURNS)
    chunks = nodes * turns
    moved = chunks - nodes
    cols = x1.shape[3] // 2

    def bit(i):
        return (w // 2**i) % 2

    def swapped(i):
        return w + 2**i - 2 ** (i + 1) * bit(i)

    levels = (0, 1, wide_bits - 2, wide_bits - 1)
    b1, b2, b3, b4 = (bit(i) for i in levels)
    partner = [(swapped(i), n) for i in levels]

    def turn_of(c):
        return TURNS[c // nodes]

    coef_copies, cw_copies, rw_copies = [], {}, {}
    for c in range(chunks):
        column = pl.multiple_of(turned(n, turn_of(c)) * cols, cols)
        coef_copies.append([
            pltpu.make_async_copy(
                coef.at[c % nodes, plane, :, pl.ds(column, cols)],
                x1.at[c, b1, :, plane * cols:(plane + 1) * cols],
                coef_sem.at[c, plane],
            )
            for plane in range(2)
        ])
    for level in range(2):
        for k in range(nodes):
            cw_copies[level, k] = pltpu.make_async_copy(colw.at[level, k], cw.at[level, k], cw_sem.at[level, k])
        for c in range(chunks):
            node = turned(n, turn_of(c)) * nodes + c % nodes
            rw_copies[level, c] = pltpu.make_async_copy(roww.at[level, node], rw.at[level, c], rw_sem.at[level, c])

    for pair in coef_copies[:AHEAD]:
        for copy in pair:
            copy.start()
    barrier = pltpu.get_barrier_semaphore()
    greeted = partner + [(w, turned(n, turn)) for turn in range(1, turns)]
    for device in greeted:
        pl.semaphore_signal(barrier, inc=1, device_id=device, device_id_type=MESH)
    for k in range(nodes):
        cw_copies[0, k].start()
    for pair in coef_copies[AHEAD:]:
        for copy in pair:
            copy.start()
    for k in range(nodes):
        cw_copies[1, k].start()
    for c in range(chunks):
        for level in range(2):
            rw_copies[level, c].start()
    pl.semaphore_wait(barrier, len(greeted))

    def exchange(stage_index, c, src, dst, device):
        return pltpu.make_async_remote_copy(
            src_ref=src,
            dst_ref=dst,
            send_sem=send.at[stage_index, c],
            recv_sem=recv.at[stage_index, c],
            device_id=device,
            device_id_type=MESH,
        )

    ex1 = [exchange(0, c, x1.at[c, b1], x1.at[c, b1], partner[0]) for c in range(chunks)]
    ex2 = [exchange(1, c, x2.at[c, b2], x2.at[c, b2], partner[1]) for c in range(chunks)]
    relay = [
        exchange(2, c, stage.at[c], x3.at[c, b3], (w, turned(n, turn_of(c)))) for c in range(moved)
    ]
    ex3 = [exchange(3, c, x3.at[c, b3], x3.at[c, b3], partner[2]) for c in range(chunks)]
    ex4 = [exchange(4, c, x4.at[c, b4], x4.at[c, b4], partner[3]) for c in range(chunks)]
    out_copies = []

    def begin(c):
        for copy in coef_copies[c]:
            copy.wait()
        ex1[c].start()

    def into(ref, *index):
        def store(real, imag):
            ref[(*index, slice(None), slice(0, cols))] = real
            ref[(*index, slice(None), slice(cols, 2 * cols))] = imag
        return store

    for c in range(AHEAD):
        begin(c)
    for step, c in events(chunks, moved):
        k = c % nodes
        if step == 1:
            if c + AHEAD < chunks:
                begin(c + AHEAD)
            if c < nodes:
                cw_copies[0, k].wait()
            ex1[c].wait_recv()
            multiply(cw.at[0, k], x1.at[c], into(x2, c, b2))
            ex2[c].start()
        elif step == 2:
            if c < nodes:
                cw_copies[1, k].wait()
            ex2[c].wait_recv()
            if c < moved:
                multiply(cw.at[1, k], x2.at[c], into(stage, c))
                relay[c].start()
            else:
                multiply(cw.at[1, k], x2.at[c], into(x3, c, b3))
                ex3[c].start()
        elif step == 3:
            relay[c].wait_recv()
            ex3[c].start()
        elif step == 4:
            rw_copies[0, c].wait()
            ex3[c].wait_recv()
            multiply(rw.at[0, c], x3.at[c], into(x4, c, b4))
            ex4[c].start()
        else:
            rw_copies[1, c].wait()
            ex4[c].wait_recv()
            multiply(rw.at[1, c], x4.at[c], into(done, c))
            node = turned(n, turn_of(c)) * nodes + k
            for plane in range(2):
                copy = pltpu.make_async_copy(
                    done.at[c, :, plane * cols:(plane + 1) * cols], out.at[node, plane], out_sem.at[c, plane]
                )
                copy.start()
                out_copies.append(copy)
    for copy in ex1 + ex2 + relay + ex3 + ex4:
        copy.wait_send()
    for copy in out_copies:
        copy.wait()


def solution(mesh):
    narrow = mesh.shape["narrow"]
    wide_bits = mesh.shape["wide"].bit_length() - 1

    def per_device(coefficients, col_weights, row_weights):
        nodes, _, rank, count = coefficients.shape
        cols = count // narrow
        chunks = nodes * narrow
        block = (chunks, 2, rank, 2 * cols)
        dtype = jnp.bfloat16
        flops = 4 * chunks * 2 * 2 * rank * 2 * rank * 2 * cols
        moved = 2 * (coefficients.size * 2 + col_weights.size + row_weights.size)
        dma = pltpu.SemaphoreType.DMA
        return pl.pallas_call(
            functools.partial(kernel, wide_bits),
            out_shape=jax.ShapeDtypeStruct((chunks, 2, rank, cols), dtype),
            in_specs=[pl.BlockSpec(memory_space=pl.ANY)] * 3,
            out_specs=pl.BlockSpec(memory_space=pl.ANY),
            scratch_shapes=[
                pltpu.VMEM(block, dtype),
                pltpu.VMEM(block, dtype),
                pltpu.VMEM(block, dtype),
                pltpu.VMEM(block, dtype),
                pltpu.VMEM((chunks - nodes, rank, 2 * cols), dtype),
                pltpu.VMEM((chunks, rank, 2 * cols), dtype),
                pltpu.VMEM((2, nodes, 2, rank, 2 * rank), dtype),
                pltpu.VMEM((2, chunks, 2, rank, 2 * rank), dtype),
                dma((chunks, 2)),
                dma((2, nodes)),
                dma((2, chunks)),
                dma((chunks, 2)),
                dma((5, chunks)),
                dma((5, chunks)),
            ],
            compiler_params=pltpu.CompilerParams(
                collective_id=0, has_side_effects=True, vmem_limit_bytes=60 * 2**20
            ),
            cost_estimate=pl.CostEstimate(flops=flops, bytes_accessed=moved, transcendentals=0),
        )(coefficients, col_weights, row_weights)

    return jax.shard_map(
        per_device,
        mesh=mesh,
        in_specs=(
            P(("wide", "narrow"), None, None, None),
            P(None, ("wide", "narrow"), None, None, None),
            P(None, "wide", None, None, None),
        ),
        out_specs=P("wide", None, None, "narrow"),
        check_vma=False,
    )
```

time: 132 us -> 79.5 us (0.60)
  waiting for transfers between devices: 87.6 us -> 0 us
  Pallas kernels: 0 us -> 77 us
  local copies, waits for them, and re-layouts: 15.4 us -> 2.3 us
  starting transfers between devices: 13 us -> 0 us
  other arithmetic: 8.39 us -> 0 us
  matrix products: 7.42 us -> 0 us
    ppermute x4 -> x0, waiting for transfers between devices: 80.9 us -> none  [swapped(): lax.ppermute(array, axis, [(i, i ^ 1 << apart) for i in range(lax.axis_si...]
    pallas_call x0 -> x1, Pallas kernels: none -> 77 us  [per_device(): pl.pallas_call(functools.partial(kernel, wide_bits), out_shape=jax.ShapeD...]
    ppermute x4 -> x0, starting transfers between devices: 9.45 us -> none  [swapped(): lax.ppermute(array, axis, [(i, i ^ 1 << apart) for i in range(lax.axis_si...]
    dot_general x16 -> x0, matrix products: 7.42 us -> none  [the longest x8 3.71 us: planes(): jnp.einsum('kab,kbn->kan', weights[:, 1], merged, preferred_element_type=...]
    all_to_all x1 -> x0, waiting for transfers between devices: 6.72 us -> none  [per_device(): lax.all_to_all(state, 'narrow', split_axis=3, concat_axis=0, tiled=True)]
    select_n x4 -> x0, other arithmetic: 5.14 us -> none  [combine(): other_weights = jnp.where(upper, weights[..., :rank], weights[..., rank:])]
    squeeze x8 -> x0, local copies, waits for them, and re-layouts: 4.42 us -> none  [the longest x1 3.8 us: per_device(): row_sets = [row_weights[0], row_weights[1]]]
    slice x2 -> x0, local copies, waits for them, and re-layouts: 4.09 us -> none  [the longest x1 3.87 us: per_device(): row_sets = [row_weights[0], row_weights[1]]]
  transfers between devices with their start and end apart: 5 -> 0, of which waited for: 5 -> 0; matrix products, arithmetic and copies ran while one was open for 13% -> 0% of each run, Pallas kernels for 0% -> 0%
where the time goes in v1:
time: 79.5 us; the launch traced here: 79.3 us
  Pallas kernels  77 us (97%)
  local copies, waits for them, and re-layouts  2.3 us (3%)
    pallas_call x1, Pallas kernels, per_device(): pl.pallas_call(functools.partial(kernel, wide_bits), out_shape=jax.ShapeD...  77 us
    unnamed x1, local copies, waits for them, and re-layouts  2.3 us

profile of v1, /device:TPU:64, one launch (start us, length us, event | category | flops | bytes accessed | tf_op | source)
XLA Modules:
  0.0 79.3 jit_solution(8652951293448117622)
XLA Ops:
  0.0 77.0 %shard_map.37 = bf16[8,2,256,128]{3,2,1,0:T(8,128)(2,1)} custom-call(bf16[2,2,256,512]{3,2,1,0:T(8,128)(2,1)} %coef.1, bf16[2,2,2,256,512]{4,3,2,1,0:T(8,128)(2,1)} %colw.1, bf16[2,8,2,256,512]{4,3,2,1,0:T(8,128)(2,1)} %roww.1), custom_call_target="tpu_custom_call" | custom-call | flops 4294967296 | bytes 12582912 | tf_op jit(solution)/shard_map/pallas_call | solution.py:201
  77.1 2.3 %copy.5 = bf16[8,2,256,128]{3,2,1,0:T(8,128)(2,1)} copy(bf16[8,2,256,128]{3,2,1,0:T(8,128)(2,1)} %shard_map.37) | data formatting | bytes 2097152

commit v2 on v1

v2 whole, which is shorter than its diff:
```python
import functools

import jax
import jax.numpy as jnp
from jax import lax
from jax.experimental import pallas as pl
from jax.experimental.pallas import tpu as pltpu
from jax.sharding import PartitionSpec as P

MESH = pl.DeviceIdType.MESH
TURNS = (0, 3, 2, 1)
AHEAD = 1
PARTS = 2
LAGS = (2.05, 1.6, 2.6)


def turned(index, turn):
    if turn == 0:
        return index
    if turn == 1:
        return index + 1 - 2 * (index % 2)
    if turn == 2:
        return index + 2 - 4 * (index // 2)
    return 3 - index


def halves(width):
    return lax.broadcasted_iota(jnp.int32, (1, width), 1) < width // 2


def crossed(array):
    return pltpu.roll(array, array.shape[1] // 2, 1)


def product(weights, block):
    merged = block[...].reshape(weights.shape[2], block.shape[2])
    first = jnp.dot(weights[0], merged, preferred_element_type=jnp.float32)
    second = crossed(jnp.dot(weights[1], merged, preferred_element_type=jnp.float32))
    return jnp.where(halves(merged.shape[1]), first - second, first + second)


def traded(a, b):
    left = halves(a.shape[1])
    return jnp.where(left, a, crossed(b)), jnp.where(left, crossed(a), b)


def events(chunks):
    expected = (0, LAGS[0], LAGS[0] + LAGS[1], sum(LAGS))
    return [(level, c) for _, level, c in sorted((c + late, level, c) for c in range(chunks) for level, late in enumerate(expected))]


def kernel(wide_bits, coef, colw, roww, out, blocks, x1, x2, x3, x4, stage, done, cw, rw,
           coef_sem, cw_sem, rw_sem, out_sem, send, recv):
    w = lax.axis_index("wide")
    n = lax.axis_index("narrow")
    nodes = coef.shape[0]
    turns = len(TURNS)
    pairs = nodes * turns
    chunks = pairs * PARTS
    cols = blocks.shape[3]

    def bit(i):
        return (w // 2**i) % 2

    def swapped(i):
        return w + 2**i - 2 ** (i + 1) * bit(i)

    levels = (0, 1, wide_bits - 2, wide_bits - 1)
    b1, b2, b3, b4 = (bit(i) for i in levels)
    partner = [(swapped(i), n) for i in levels]

    def turn_of(pair):
        return TURNS[pair // nodes]

    coef_copies, cw_copies, rw_copies = [], {}, {}
    for pair in range(pairs):
        column = pl.multiple_of(turned(n, turn_of(pair)) * cols, cols)
        coef_copies.append([
            pltpu.make_async_copy(
                coef.at[pair % nodes, plane, :, pl.ds(column, cols)], blocks.at[pair, plane], coef_sem.at[pair, plane]
            )
            for plane in range(2)
        ])
    for level in range(2):
        for k in range(nodes):
            cw_copies[level, k] = pltpu.make_async_copy(colw.at[level, k], cw.at[level, k], cw_sem.at[level, k])
        for pair in range(pairs):
            node = turned(n, turn_of(pair)) * nodes + pair % nodes
            rw_copies[level, pair] = pltpu.make_async_copy(roww.at[level, node], rw.at[level, pair], rw_sem.at[level, pair])

    for pair in coef_copies:
        for copy in pair:
            copy.start()
    barrier = pltpu.get_barrier_semaphore()
    across = partner[2][0]
    greeted = partner + [(row, turned(n, turn)) for turn in range(1, turns) for row in (w, across)]
    for device in greeted:
        pl.semaphore_signal(barrier, inc=1, device_id=device, device_id_type=MESH)
    for level in range(2):
        for k in range(nodes):
            cw_copies[level, k].start()

    def exchange(stage_index, c, src, dst, device):
        return pltpu.make_async_remote_copy(
            src_ref=src,
            dst_ref=dst,
            send_sem=send.at[stage_index, c],
            recv_sem=recv.at[stage_index, c],
            device_id=device,
            device_id_type=MESH,
        )

    ex1 = [exchange(0, c, x1.at[c, b1], x1.at[c, b1], partner[0]) for c in range(chunks)]
    ex2 = [exchange(1, c, x2.at[c, b2], x2.at[c, b2], partner[1]) for c in range(chunks)]
    relay, ex3 = {}, []
    for c in range(chunks):
        turn = turn_of(c // PARTS)
        owner = turned(n, turn)
        source = stage.at[c] if turn else x3.at[c, b3]
        if turn:
            relay[c] = exchange(2, c, source, x3.at[c, b3], (w, owner))
        ex3.append(exchange(3, c, source, x3.at[c, b3], (across, owner)))
    ex4 = [exchange(4, c, x4.at[c, b4], x4.at[c, b4], partner[3]) for c in range(chunks)]
    out_copies = []

    def prepare(pair):
        for copy in coef_copies[pair]:
            copy.wait()
        parts = traded(blocks[pair, 0].astype(jnp.float32), blocks[pair, 1].astype(jnp.float32))
        for part in range(PARTS):
            x1[pair * PARTS + part, b1] = parts[part].astype(jnp.bfloat16)

    def begin(c):
        if c % PARTS == 0 and c > 0:
            prepare(c // PARTS)
        ex1[c].start()

    prepare(0)
    pl.semaphore_wait(barrier, len(greeted))
    for c in range(AHEAD):
        begin(c)
    for pair in range(pairs):
        for level in range(2):
            rw_copies[level, pair].start()
    for step, c in events(chunks):
        pair, part = c // PARTS, c % PARTS
        k = pair % nodes
        if step == 0:
            if c + AHEAD < chunks:
                begin(c + AHEAD)
            if pair < nodes and part == 0:
                cw_copies[0, k].wait()
            ex1[c].wait_recv()
            x2[c, b2] = product(cw.at[0, k], x1.at[c]).astype(jnp.bfloat16)
            ex2[c].start()
        elif step == 1:
            if pair < nodes and part == 0:
                cw_copies[1, k].wait()
            ex2[c].wait_recv()
            if c in relay:
                stage[c] = product(cw.at[1, k], x2.at[c]).astype(jnp.bfloat16)
                ex3[c].start()
                relay[c].start()
            else:
                x3[c, b3] = product(cw.at[1, k], x2.at[c]).astype(jnp.bfloat16)
                ex3[c].start()
        elif step == 2:
            if part == 0:
                rw_copies[0, pair].wait()
            if c in relay:
                relay[c].wait_recv()
            ex3[c].wait_recv()
            x4[c, b4] = product(rw.at[0, pair], x3.at[c]).astype(jnp.bfloat16)
            ex4[c].start()
        else:
            if part == 0:
                rw_copies[1, pair].wait()
            ex4[c].wait_recv()
            result = product(rw.at[1, pair], x4.at[c])
            if part == 0:
                done[pair, 0] = result.astype(jnp.bfloat16)
            else:
                node = turned(n, turn_of(pair)) * nodes + k
                for plane, value in enumerate(traded(done[pair, 0].astype(jnp.float32), result)):
                    done[pair, plane] = value.astype(jnp.bfloat16)
                copy = pltpu.make_async_copy(done.at[pair], out.at[node], out_sem.at[pair])
                copy.start()
                out_copies.append(copy)
    for copy in ex1 + ex2 + list(relay.values()) + ex3 + ex4:
        copy.wait_send()
    for copy in out_copies:
        copy.wait()


def solution(mesh):
    narrow = mesh.shape["narrow"]
    wide_bits = mesh.shape["wide"].bit_length() - 1

    def per_device(coefficients, col_weights, row_weights):
        nodes, _, rank, count = coefficients.shape
        cols = count // narrow
        pairs = nodes * narrow
        chunks = pairs * PARTS
        block = (chunks, 2, rank, cols)
        dtype = jnp.bfloat16
        flops = 4 * pairs * 2 * 2 * rank * 2 * rank * 2 * cols
        moved = 2 * (coefficients.size * 2 + col_weights.size + row_weights.size)
        dma = pltpu.SemaphoreType.DMA
        return pl.pallas_call(
            functools.partial(kernel, wide_bits),
            out_shape=jax.ShapeDtypeStruct((pairs, 2, rank, cols), dtype),
            in_specs=[pl.BlockSpec(memory_space=pl.ANY)] * 3,
            out_specs=pl.BlockSpec(memory_space=pl.ANY),
            scratch_shapes=[
                pltpu.VMEM((pairs, 2, rank, cols), dtype),
                pltpu.VMEM(block, dtype),
                pltpu.VMEM(block, dtype),
                pltpu.VMEM(block, dtype),
                pltpu.VMEM(block, dtype),
                pltpu.VMEM((chunks, rank, cols), dtype),
                pltpu.VMEM((pairs, 2, rank, cols), dtype),
                pltpu.VMEM((2, nodes, 2, rank, 2 * rank), dtype),
                pltpu.VMEM((2, pairs, 2, rank, 2 * rank), dtype),
                dma((pairs, 2)),
                dma((2, nodes)),
                dma((2, pairs)),
                dma((pairs,)),
                dma((5, chunks)),
                dma((5, chunks)),
            ],
            compiler_params=pltpu.CompilerParams(
                collective_id=0, has_side_effects=True, vmem_limit_bytes=60 * 2**20
            ),
            cost_estimate=pl.CostEstimate(flops=flops, bytes_accessed=moved, transcendentals=0),
        )(coefficients, col_weights, row_weights)

    return jax.shard_map(
        per_device,
        mesh=mesh,
        in_specs=(
            P(("wide", "narrow"), None, None, None),
            P(None, ("wide", "narrow"), None, None, None),
            P(None, "wide", None, None, None),
        ),
        out_specs=P("wide", None, None, "narrow"),
        check_vma=False,
    )
```

time: 79.5 us -> 72.5 us (0.912)
  Pallas kernels: 77 us -> 69.6 us
    pallas_call x1, Pallas kernels: 77 us -> 69.6 us  [per_device(): pl.pallas_call(functools.partial(kernel, wide_bits), out_shape=jax.ShapeD...]
where the time goes in v2:
time: 72.5 us; the launch traced here: 71.9 us
  Pallas kernels  69.6 us (96%)
  local copies, waits for them, and re-layouts  2.3 us (3%)
    pallas_call x1, Pallas kernels, per_device(): pl.pallas_call(functools.partial(kernel, wide_bits), out_shape=jax.ShapeD...  69.6 us
    unnamed x1, local copies, waits for them, and re-layouts  2.3 us

profile of v2, /device:TPU:64, one launch (start us, length us, event | category | flops | bytes accessed | tf_op | source)
XLA Modules:
  0.0 71.9 jit_solution(12906799710409536370)
XLA Ops:
  0.0 69.6 %shard_map.37 = bf16[8,2,256,128]{3,2,1,0:T(8,128)(2,1)} custom-call(bf16[2,2,256,512]{3,2,1,0:T(8,128)(2,1)} %coef.1, bf16[2,2,2,256,512]{4,3,2,1,0:T(8,128)(2,1)} %colw.1, bf16[2,8,2,256,512]{4,3,2,1,0:T(8,128)(2,1)} %roww.1), custom_call_target="tpu_custom_call" | custom-call | flops 4294967296 | bytes 12582912 | tf_op jit(solution)/shard_map/pallas_call | solution.py:209
  69.6 2.3 %copy.5 = bf16[8,2,256,128]{3,2,1,0:T(8,128)(2,1)} copy(bf16[8,2,256,128]{3,2,1,0:T(8,128)(2,1)} %shard_map.37) | data formatting | bytes 2097152

commit v3 on v2

v3 whole, which is shorter than its diff:
```python
import functools

import jax
import jax.numpy as jnp
from jax import lax
from jax.experimental import pallas as pl
from jax.experimental.pallas import tpu as pltpu
from jax.sharding import PartitionSpec as P

MESH = pl.DeviceIdType.MESH
AHEAD = 1
PARTS = 2
LAGS = (2.05, 1.6, 2.6)
VMEM_LIMIT = 52


def turned(index, turn):
    if turn == 0:
        return index
    if turn == 1:
        return index + 1 - 2 * (index % 2)
    if turn == 2:
        return index + 2 - 4 * (index // 2)
    return 3 - index


def halves(width):
    return lax.broadcasted_iota(jnp.int32, (1, width), 1) < width // 2


def crossed(array):
    return pltpu.roll(array, array.shape[1] // 2, 1)


def product(weights, block):
    merged = block[...].reshape(weights.shape[2], block.shape[2])
    first = jnp.dot(weights[0], merged, preferred_element_type=jnp.float32)
    second = crossed(jnp.dot(weights[1], merged, preferred_element_type=jnp.float32))
    return jnp.where(halves(merged.shape[1]), first - second, first + second)


def traded(a, b):
    left = halves(a.shape[1])
    return jnp.where(left, a, crossed(b)), jnp.where(left, crossed(a), b)


def plan(nodes):
    stay = [(turn, k, part) for turn in (0, 1) for k in range(nodes) for part in range(PARTS)]
    leave = [(turn, k, part) for turn in (3, 2) for k in range(nodes) for part in range(PARTS)]
    half = len(stay) // 2
    chunks = []
    for i in range(len(stay)):
        chunks += (stay[i], leave[i]) if i < half else (leave[i], stay[i])
    return chunks


def events(chunks):
    expected = (0, LAGS[0], LAGS[0] + LAGS[1], sum(LAGS))
    return [(level, c) for _, level, c in sorted((c + late, level, c) for c in range(chunks) for level, late in enumerate(expected))]


def kernel(wide_bits, coef, colw, roww, out, blocks, x1, x2, x3, x4, stage, held, cw, rw,
           coef_sem, cw_sem, rw_sem, send, recv):
    w = lax.axis_index("wide")
    n = lax.axis_index("narrow")
    nodes = coef.shape[0]
    order = plan(nodes)
    chunks = len(order)
    pairs = list(dict.fromkeys((turn, k) for turn, k, _ in order))
    pair_of = [pairs.index(chunk[:2]) for chunk in order]
    members = [[c for c in range(chunks) if pair_of[c] == pair] for pair in range(len(pairs))]
    cols = blocks.shape[3]

    def bit(i):
        return (w // 2**i) % 2

    def swapped(i):
        return w + 2**i - 2 ** (i + 1) * bit(i)

    levels = (0, 1, wide_bits - 2, wide_bits - 1)
    b1, b2, b3, b4 = (bit(i) for i in levels)
    partner = [(swapped(i), n) for i in levels]

    coef_copies, rw_copies = [], []
    for pair, (turn, k) in enumerate(pairs):
        owner = turned(n, turn)
        column = pl.multiple_of(owner * cols, cols)
        coef_copies.append(pltpu.make_async_copy(coef.at[k, :, :, pl.ds(column, cols)], blocks.at[pair], coef_sem.at[pair]))
        rw_copies.append(pltpu.make_async_copy(roww.at[:, owner * nodes + k], rw.at[:, pair], rw_sem.at[pair]))
    cw_copies = [pltpu.make_async_copy(colw.at[:, k], cw.at[:, k], cw_sem.at[k]) for k in range(nodes)]

    for copy in coef_copies:
        copy.start()
    barrier = pltpu.get_barrier_semaphore()
    across = partner[2][0]
    greeted = partner + [(row, turned(n, turn)) for turn in (1, 2, 3) for row in (w, across)]
    for device in greeted:
        pl.semaphore_signal(barrier, inc=1, device_id=device, device_id_type=MESH)
    for copy in cw_copies:
        copy.start()

    def exchange(stage_index, c, src, dst, device):
        return pltpu.make_async_remote_copy(
            src_ref=src,
            dst_ref=dst,
            send_sem=send.at[stage_index],
            recv_sem=recv.at[stage_index, c],
            device_id=device,
            device_id_type=MESH,
        )

    ex1 = [exchange(0, c, x1.at[c, b1], x1.at[c, b1], partner[0]) for c in range(chunks)]
    ex2 = [exchange(1, c, x2.at[c, b2], x2.at[c, b2], partner[1]) for c in range(chunks)]
    relay, ex3 = {}, []
    for c, (turn, _, _) in enumerate(order):
        owner = turned(n, turn)
        source = stage.at[c] if turn else x3.at[c, b3]
        if turn:
            relay[c] = exchange(2, c, source, x3.at[c, b3], (w, owner))
        ex3.append(exchange(3, c, source, x3.at[c, b3], (across, owner)))
    ex4 = [exchange(4, c, x4.at[c, b4], x4.at[c, b4], partner[3]) for c in range(chunks)]

    def prepare(pair):
        coef_copies[pair].wait()
        parts = traded(blocks[pair, 0].astype(jnp.float32), blocks[pair, 1].astype(jnp.float32))
        for c, part in zip(members[pair], parts, strict=True):
            x1[c, b1] = part.astype(jnp.bfloat16)

    def begin(c):
        if c == members[pair_of[c]][0] and c > 0:
            prepare(pair_of[c])
        ex1[c].start()

    prepare(0)
    pl.semaphore_wait(barrier, len(greeted))
    for c in range(AHEAD):
        begin(c)
    for copy in rw_copies:
        copy.start()
    unread = {"cw": set(range(nodes)), "rw": set(range(len(pairs)))}

    def loaded(name, i):
        if i in unread[name]:
            unread[name].remove(i)
            (cw_copies if name == "cw" else rw_copies)[i].wait()

    for step, c in events(chunks):
        pair = pair_of[c]
        k = pairs[pair][1]
        if step == 0:
            if c + AHEAD < chunks:
                begin(c + AHEAD)
            loaded("cw", k)
            ex1[c].wait_recv()
            x2[c, b2] = product(cw.at[0, k], x1.at[c]).astype(jnp.bfloat16)
            ex2[c].start()
        elif step == 1:
            ex2[c].wait_recv()
            if c in relay:
                stage[c] = product(cw.at[1, k], x2.at[c]).astype(jnp.bfloat16)
                ex3[c].start()
                relay[c].start()
            else:
                x3[c, b3] = product(cw.at[1, k], x2.at[c]).astype(jnp.bfloat16)
                ex3[c].start()
        elif step == 2:
            loaded("rw", pair)
            if c in relay:
                relay[c].wait_recv()
            ex3[c].wait_recv()
            x4[c, b4] = product(rw.at[0, pair], x3.at[c]).astype(jnp.bfloat16)
            ex4[c].start()
        else:
            ex4[c].wait_recv()
            result = product(rw.at[1, pair], x4.at[c])
            if c == members[pair][0]:
                held[pair] = result.astype(jnp.bfloat16)
            else:
                node = turned(n, pairs[pair][0]) * nodes + k
                for plane, value in enumerate(traded(held[pair].astype(jnp.float32), result)):
                    out[node, plane] = value.astype(jnp.bfloat16)
    for i, (sent, copies) in enumerate(((x1, ex1), (x2, ex2), (stage, relay), (x3, ex3), (x4, ex4))):
        whole = sent if sent is stage else sent.at[:, 0]
        whole = whole.at[pl.ds(0, len(copies))]
        pltpu.make_async_copy(whole, whole, send.at[i]).wait()


def solution(mesh):
    narrow = mesh.shape["narrow"]
    wide_bits = mesh.shape["wide"].bit_length() - 1

    def per_device(coefficients, col_weights, row_weights):
        nodes, _, rank, count = coefficients.shape
        cols = count // narrow
        pairs = nodes * narrow
        chunks = pairs * PARTS
        block = (chunks, 2, rank, cols)
        dtype = jnp.bfloat16
        flops = 4 * pairs * 2 * 2 * rank * 2 * rank * 2 * cols
        moved = 2 * (coefficients.size * 2 + col_weights.size + row_weights.size)
        dma = pltpu.SemaphoreType.DMA
        return pl.pallas_call(
            functools.partial(kernel, wide_bits),
            out_shape=jax.ShapeDtypeStruct((pairs, 2, rank, cols), dtype),
            in_specs=[pl.BlockSpec(memory_space=pl.ANY)] * 3,
            out_specs=pl.BlockSpec(memory_space=pltpu.VMEM),
            scratch_shapes=[
                pltpu.VMEM((pairs, 2, rank, cols), dtype),
                pltpu.VMEM(block, dtype),
                pltpu.VMEM(block, dtype),
                pltpu.VMEM(block, dtype),
                pltpu.VMEM(block, dtype),
                pltpu.VMEM((chunks, rank, cols), dtype),
                pltpu.VMEM((pairs, rank, cols), dtype),
                pltpu.VMEM((2, nodes, 2, rank, 2 * rank), dtype),
                pltpu.VMEM((2, pairs, 2, rank, 2 * rank), dtype),
                dma((pairs,)),
                dma((nodes,)),
                dma((pairs,)),
                dma((5,)),
                dma((5, chunks)),
            ],
            compiler_params=pltpu.CompilerParams(
                collective_id=0, has_side_effects=True, vmem_limit_bytes=VMEM_LIMIT * 2**20
            ),
            cost_estimate=pl.CostEstimate(flops=flops, bytes_accessed=moved, transcendentals=0),
        )(coefficients, col_weights, row_weights)

    return jax.shard_map(
        per_device,
        mesh=mesh,
        in_specs=(
            P(("wide", "narrow"), None, None, None),
            P(None, ("wide", "narrow"), None, None, None),
            P(None, "wide", None, None, None),
        ),
        out_specs=P("wide", None, None, "narrow"),
        check_vma=False,
    )
```

time: 72.5 us -> 69.6 us (0.960)
  local copies, waits for them, and re-layouts: 2.3 us -> 0.97 us
  Pallas kernels: 69.6 us -> 68.5 us
    unnamed x1, local copies, waits for them, and re-layouts: 2.3 us -> 0.97 us
    pallas_call x1, Pallas kernels: 69.6 us -> 68.5 us  [per_device(): pl.pallas_call(functools.partial(kernel, wide_bits), out_shape=jax.ShapeD...]
where the time goes in v3:
time: 69.6 us; the launch traced here: 69.5 us
  Pallas kernels  68.5 us (98%)
  local copies, waits for them, and re-layouts  0.97 us (1%)
    pallas_call x1, Pallas kernels, per_device(): pl.pallas_call(functools.partial(kernel, wide_bits), out_shape=jax.ShapeD...  68.5 us

profile of v3, /device:TPU:64, one launch (start us, length us, event | category | flops | bytes accessed | tf_op | source)
XLA Modules:
  0.0 69.5 jit_solution(4044852946241123408)
XLA Ops:
  0.0 68.5 %shard_map.37 = bf16[8,2,256,128]{3,2,1,0:T(8,128)(2,1)S(1)} custom-call(bf16[2,2,256,512]{3,2,1,0:T(8,128)(2,1)} %coef.1, bf16[2,2,2,256,512]{4,3,2,1,0:T(8,128)(2,1)} %colw.1, bf16[2,8,2,256,512]{4,3,2,1,0:T(8,128)(2,1)} %roww.1), custom_call_target="tpu_custom_call" | custom-call | flops 4294967296 | bytes 12582912 | tf_op jit(solution)/shard_map/pallas_call | solution.py:202
  68.5 1.0 %copy.5 = bf16[8,2,256,128]{3,2,1,0:T(8,128)(2,1)} copy(bf16[8,2,256,128]{3,2,1,0:T(8,128)(2,1)S(1)} %shard_map.37) | data formatting | bytes 2097152

commit v4 on v3

--- a/solution.py
+++ b/solution.py
@@ -8,7 +8,8 @@
 from jax.sharding import PartitionSpec as P
 
 MESH = pl.DeviceIdType.MESH
-AHEAD = 1
+AHEAD = 2
+SLOTS = 8
 PARTS = 2
 LAGS = (2.05, 1.6, 2.6)
 VMEM_LIMIT = 52
@@ -99,12 +100,17 @@
     for copy in cw_copies:
         copy.start()
 
+    def landed(stage_index, c):
+        if stage_index in (2, 3):
+            return recv.at[3 * SLOTS + (stage_index - 2) * chunks + c]
+        return recv.at[(0, 1, None, None, 2)[stage_index] * SLOTS + c % SLOTS]
+
     def exchange(stage_index, c, src, dst, device):
         return pltpu.make_async_remote_copy(
             src_ref=src,
             dst_ref=dst,
             send_sem=send.at[stage_index],
-            recv_sem=recv.at[stage_index, c],
+            recv_sem=landed(stage_index, c),
             device_id=device,
             device_id_type=MESH,
         )
@@ -218,7 +224,7 @@
                 dma((nodes,)),
                 dma((pairs,)),
                 dma((5,)),
-                dma((5, chunks)),
+                dma((3 * SLOTS + 2 * chunks,)),
             ],
             compiler_params=pltpu.CompilerParams(
                 collective_id=0, has_side_effects=True, vmem_limit_bytes=VMEM_LIMIT * 2**20

time: 69.6 us -> 69.2 us (level)
  no operation moved by 1% of the time
where the time goes in v4:
time: 69.2 us; the launch traced here: 69.1 us
  Pallas kernels  68.1 us (98%)
  local copies, waits for them, and re-layouts  0.97 us (1%)
    pallas_call x1, Pallas kernels, per_device(): pl.pallas_call(functools.partial(kernel, wide_bits), out_shape=jax.ShapeD...  68.1 us

profile of v4, /device:TPU:64, one launch (start us, length us, event | category | flops | bytes accessed | tf_op | source)
XLA Modules:
  0.0 69.1 jit_solution(13946089339512645275)
XLA Ops:
  0.0 68.1 %shard_map.37 = bf16[8,2,256,128]{3,2,1,0:T(8,128)(2,1)S(1)} custom-call(bf16[2,2,256,512]{3,2,1,0:T(8,128)(2,1)} %coef.1, bf16[2,2,2,256,512]{4,3,2,1,0:T(8,128)(2,1)} %colw.1, bf16[2,8,2,256,512]{4,3,2,1,0:T(8,128)(2,1)} %roww.1), custom_call_target="tpu_custom_call" | custom-call | flops 4294967296 | bytes 12582912 | tf_op jit(solution)/shard_map/pallas_call | solution.py:208
  68.1 1.0 %copy.5 = bf16[8,2,256,128]{3,2,1,0:T(8,128)(2,1)} copy(bf16[8,2,256,128]{3,2,1,0:T(8,128)(2,1)S(1)} %shard_map.37) | data formatting | bytes 2097152
